TPU v7x, 32 devices: a whole 2x2x4 slice. The times are simulated.
32 devices in a mesh: row: 4 (over y, x), col: 8 (over z, core).
Axes of the slice: x: 2, y: 2, z: 4, core: 2. Of those that a mesh axis runs over, the one named last changes fastest.
Arguments:
- vorticity: float32 [3, 128, 128, 128], P(None, 'row', 'col'), may hold values from -18.1 to 18.1
- scalar: float32 [256, 256, 256], P('row', 'col'), may hold values from -6 to 6
Outputs:
- advected: float32 [256, 256, 256], P('row', 'col')
All inputs are finite; a program needn't handle non-finite values. Where the computation divides by a largest or mean magnitude, that divisor is 1e-20 or more.
Results may differ from a plain program's by a relative error of at most 0.0003.
Values sent between devices are 32-bit elements; how exact they have to be, the bound alone decides.
A program may use at most 128 MiB of HBM per device.

v0:
```python
import math
import jax
import jax.numpy as jnp
from jax import lax
from jax.sharding import PartitionSpec as P

COURANT = 0.9
EPSILON = 1e-06
HIGHEST = lax.Precision.HIGHEST


def with_halo(cells, sides, width):
    for axis, dim in sides:
        count = lax.axis_size(axis)
        head = lax.slice_in_dim(cells, 0, width, axis=dim)
        tail = lax.slice_in_dim(cells, cells.shape[dim] - width, cells.shape[dim], axis=dim)
        cells = jnp.concatenate(
            [
                lax.ppermute(tail, axis, [(i, (i + 1) % count) for i in range(count)]),
                cells,
                lax.ppermute(head, axis, [((i + 1) % count, i) for i in range(count)]),
            ],
            axis=dim,
        )
    return cells


def kernel_weight(distance):
    radius = jnp.abs(distance)
    inner_lobe = (
        -(radius - 1.0)
        * ((((25.0 * radius - 38.0) * radius - 3.0) * radius + 12.0) * radius + 12.0)
        / 12.0
    )
    middle_lobe = (
        (radius - 1.0)
        * (radius - 2.0)
        * (((25.0 * radius - 114.0) * radius + 153.0) * radius - 48.0)
        / 24.0
    )
    outer_cube = (radius - 3.0) * (radius - 3.0) * (radius - 3.0)
    outer_lobe = -(radius - 2.0) * outer_cube * (5.0 * radius - 8.0) / 24.0
    return jnp.where(
        radius < 1.0,
        inner_lobe,
        jnp.where(radius < 2.0, middle_lobe, jnp.where(radius < 3.0, outer_lobe, 0.0)),
    )


def tables(length):
    indices = jnp.arange(length, dtype=jnp.int32)
    product = indices[:, None] * indices[None, :] % length
    angle = product.astype(jnp.float32) * (2.0 * math.pi / length)
    return (jnp.cos(angle), jnp.sin(angle))


def rotate(complex_pair, formula, cosine, sine, direction):
    real_cos = jnp.einsum(formula, complex_pair[0], cosine, precision=HIGHEST)
    real_sin = jnp.einsum(formula, complex_pair[0], sine, precision=HIGHEST)
    imag_cos = jnp.einsum(formula, complex_pair[1], cosine, precision=HIGHEST)
    imag_sin = jnp.einsum(formula, complex_pair[1], sine, precision=HIGHEST)
    return jnp.stack([real_cos - direction * imag_sin, imag_cos + direction * real_sin])


def wavenumber(start, count, length):
    indices = start + jnp.arange(count, dtype=jnp.int32)
    waves = jnp.where(indices < length // 2, indices, indices - length).astype(jnp.float32)
    return (waves, indices == length // 2)


def induce(spectrum, xwaves, ywaves, zwaves, banned, inverse_cube):
    wave_sq = xwaves * xwaves + ywaves * ywaves + zwaves * zwaves
    keep = (wave_sq > 0.0) & jnp.logical_not(banned)
    factor = jnp.where(keep, 1.0 / jnp.maximum(wave_sq, 1.0), 0.0) * inverse_cube
    crosses = []
    for part_index in range(2):
        omega = spectrum[part_index]
        crosses.append(
            jnp.stack(
                [
                    ywaves * omega[2] - zwaves * omega[1],
                    zwaves * omega[0] - xwaves * omega[2],
                    xwaves * omega[1] - ywaves * omega[0],
                ]
            )
        )
    return jnp.stack([-crosses[1] * factor, crosses[0] * factor])


def merged_shape(lower, grid_axis):
    shape = list(lower.shape)
    shape[grid_axis] = 2 * shape[grid_axis]
    return shape


def refine_roll(coarse, grid_axis):
    lower = 0.75 * coarse + 0.25 * jnp.roll(coarse, 1, grid_axis)
    upper = 0.75 * coarse + 0.25 * jnp.roll(coarse, -1, grid_axis)
    return jnp.stack([lower, upper], axis=grid_axis + 1).reshape(merged_shape(lower, grid_axis))


def refine_rim(coarse, grid_axis):
    length = coarse.shape[grid_axis]
    inner = lax.slice_in_dim(coarse, 1, length - 1, axis=grid_axis)
    below = lax.slice_in_dim(coarse, 0, length - 2, axis=grid_axis)
    above = lax.slice_in_dim(coarse, 2, length, axis=grid_axis)
    lower = 0.75 * inner + 0.25 * below
    upper = 0.75 * inner + 0.25 * above
    return jnp.stack([lower, upper], axis=grid_axis + 1).reshape(merged_shape(lower, grid_axis))


def remesh_roll(field, displace, grid_axis):
    summed = jnp.zeros(field.shape, jnp.float32)
    for offset in range(-3, 4):
        summed = summed + jnp.roll(field, offset, grid_axis) * kernel_weight(
            offset - jnp.roll(displace, offset, grid_axis)
        )
    return summed


def remesh_rim(field_ext, displace_ext, grid_axis, count):
    shape = list(field_ext.shape)
    shape[grid_axis] = count
    summed = jnp.zeros(shape, jnp.float32)
    for offset in range(-3, 4):
        begin = 3 - offset
        values = lax.slice_in_dim(field_ext, begin, begin + count, axis=grid_axis)
        moved = lax.slice_in_dim(displace_ext, begin, begin + count, axis=grid_axis)
        summed = summed + values * kernel_weight(offset - moved)
    return summed


def shards(vorticity, scalar):
    coarse_n = vorticity.shape[3]
    cos_full, sin_full = tables(coarse_n)
    mode_count = coarse_n // 2
    weights = jnp.where(jnp.arange(mode_count) == 0, 1.0, 2.0).astype(jnp.float32)
    cos_fwd = cos_full[:, :mode_count]
    sin_fwd = sin_full[:, :mode_count]
    cos_back = cos_full[:mode_count, :] * weights[:, None]
    sin_back = sin_full[:mode_count, :] * weights[:, None]
    forward = jnp.stack(
        [
            jnp.einsum("cyzx,xk->cyzk", vorticity, cos_fwd, precision=HIGHEST),
            -jnp.einsum("cyzx,xk->cyzk", vorticity, sin_fwd, precision=HIGHEST),
        ]
    )
    spectrum = rotate(
        lax.all_to_all(forward, "row", split_axis=4, concat_axis=2, tiled=True),
        "cyzk,yq->czkq",
        cos_full,
        sin_full,
        -1.0,
    )
    spectrum = rotate(
        lax.all_to_all(spectrum, "col", split_axis=4, concat_axis=2, tiled=True),
        "czkq,zw->ckqw",
        cos_full,
        sin_full,
        -1.0,
    )
    first_count = spectrum.shape[2]
    second_count = spectrum.shape[3]
    xwaves, xnyquist = wavenumber(lax.axis_index("row") * first_count, first_count, coarse_n)
    ywaves, ynyquist = wavenumber(lax.axis_index("col") * second_count, second_count, coarse_n)
    zwaves, znyquist = wavenumber(0, coarse_n, coarse_n)
    banned = xnyquist[:, None, None] | ynyquist[None, :, None] | znyquist[None, None, :]
    inverse_cube = 1.0 / (coarse_n * coarse_n * coarse_n)
    velocity_hat = induce(
        spectrum,
        xwaves[:, None, None],
        ywaves[None, :, None],
        zwaves[None, None, :],
        banned,
        inverse_cube,
    )
    inverse_z = rotate(velocity_hat, "ckqw,wz->ckqz", cos_full, sin_full, 1.0)
    mixed = rotate(
        lax.all_to_all(inverse_z, "col", split_axis=4, concat_axis=3, tiled=True),
        "ckqz,qy->ckzy",
        cos_full,
        sin_full,
        1.0,
    )
    block = lax.all_to_all(mixed, "row", split_axis=4, concat_axis=2, tiled=True)
    velocity = jnp.einsum("ckzy,kx->cyzx", block[0], cos_back, precision=HIGHEST) - jnp.einsum(
        "ckzy,kx->cyzx", block[1], sin_back, precision=HIGHEST
    )
    velocity_peak = lax.pmax(jnp.max(jnp.abs(velocity)), ("row", "col"))
    courant_scale = COURANT / (velocity_peak + EPSILON)
    fine_rows = scalar.shape[0]
    fine_cols = scalar.shape[1]
    rimmed = with_halo(velocity, (("row", 1), ("col", 2)), 1)
    displaced = refine_rim(refine_rim(refine_roll(rimmed, 3), 1), 2) * courant_scale
    swept = remesh_roll(scalar, displaced[0], 2)
    rows_input = jnp.stack([swept, displaced[1]])
    rows_ext = with_halo(rows_input, (("row", 1),), 3)
    ymoved = rows_ext[1]
    swept = remesh_rim(rows_ext[0], ymoved, 0, fine_rows)
    cols_input = jnp.stack([swept, displaced[2]])
    cols_ext = with_halo(cols_input, (("col", 2),), 3)
    zmoved = cols_ext[1]
    return remesh_rim(cols_ext[0], zmoved, 1, fine_cols)


def solution(mesh):
    in_specs = (P(None, "row", "col", None), P("row", "col", None))
    out_specs = P("row", "col", None)
    return jax.shard_map(shards, mesh=mesh, in_specs=in_specs, out_specs=out_specs, check_vma=False)
```

profile of v0, /device:TPU:1, one launch (start us, length us, event | category | flops | bytes accessed | tf_op | source)
XLA Modules:
  0.0 478.1 jit_solution(8644423327381944516)
XLA Ops:
  3.1 2.5 copy.292
  5.6 3.4 reshape.296
  9.0 14.5 %all_to_all.60 = f32[4,1,49152]{2,1,0:T(1,128)S(1)} all-to-all(f32[4,1,49152]{2,1,0:T(1,128)S(1)} %reshape.296), channel_id=1, replica_groups=mesh['row'=4,'col'=8] {'row'}, dimensions={0} | all-to-all | bytes 1572864 | tf_op jit(solution)/shard_map/all_to_all | solution.py:149
  24.0 3.0 reduce
  27.0 2.7 reshape.297
  29.7 3.7 copy.293
  35.6 2.1 squeeze.23
  40.3 2.1 squeeze.22
  44.6 6.5 %copy.296 = f32[2,3,16,16,128]{3,2,1,0,4:T(8,128)} copy(f32[2,3,16,16,128]{4,3,2,1,0:T(8,128)S(1)} %pad_maximum_fusion.7) | data formatting | bytes 1572864 | tf_op jit(solution)/shard_map/stack | solution.py:62
  51.2 5.5 %reshape.298 = f32[8,1,24576]{2,1,0:T(1,128)} reshape(f32[128,2,3,16,16]{4,3,2,1,0:T(8,128)} %bitcast.181) | data formatting | bytes 1572864
  56.6 7.0 %all-to-all-start.1 = ((f32[8,1,24576]{2,1,0:T(1,128)}), f32[8,1,24576]{2,1,0:T(1,128)S(1)}, u32[]{:S(2)}, u32[]{:S(2)}) async-start(f32[8,1,24576]{2,1,0:T(1,128)} %reshape.298), calls=%async_computation.1 | async-start | bytes 1572864 | tf_op jit(solution)/shard_map/all_to_all | solution.py:156
  64.0 19.6 %all-to-all-done.1 = f32[8,1,24576]{2,1,0:T(1,128)S(1)} async-done(((f32[8,1,24576]{2,1,0:T(1,128)}), f32[8,1,24576]{2,1,0:T(1,128)S(1)}, u32[]{:S(2)}, u32[]{:S(2)}) %all-to-all-start.1) | async-done | bytes 786464 | tf_op jit(solution)/shard_map/all_to_all | solution.py:156
  83.7 2.6 reduce.1
  86.2 4.8 reshape.299
  91.0 8.0 %copy.297 = f32[2,3,16,16,8,16]{2,4,5,3,1,0:T(8,128)} copy(f32[2,3,16,16,8,16]{3,2,1,0,5,4:T(8,128)} %bitcast.182) | data formatting | bytes 1572864 | tf_op jit(solution)/shard_map/all_to_all | solution.py:156
  99.0 6.3 %fusion.342 = (f32[1,3,8,16,16,16]{3,2,5,4,1,0:T(8,128)}, f32[1,3,8,16,16,16]{3,2,5,4,1,0:T(8,128)}) fusion(f32[2,3,8,16,16,16]{3,2,5,4,1,0:T(8,128)} %bitcast.179), kind=kLoop, calls=%fused_computation.442 | loop fusion | bytes 1572864 | tf_op jit(solution)/shard_map/slice | solution.py:59
  105.4 2.4 squeeze.25
  108.5 2.6 squeeze.24
  116.4 6.0 %copy.298 = f32[2,3,16,16,128]{3,2,1,0,4:T(8,128)} copy(f32[2,3,16,16,128]{4,3,2,1,0:T(8,128)S(1)} %pad_maximum_fusion.8) | data formatting | bytes 1572864 | tf_op jit(solution)/shard_map/stack | solution.py:62
  122.4 5.6 %reshape.300 = f32[8,1,24576]{2,1,0:T(1,128)} reshape(f32[128,2,3,16,16]{4,3,2,1,0:T(8,128)} %bitcast.183) | data formatting | bytes 1572864
  128.0 5.3 %all-to-all-start.2 = ((f32[8,1,24576]{2,1,0:T(1,128)}), f32[8,1,24576]{2,1,0:T(1,128)}, u32[]{:S(2)}, u32[]{:S(2)}) async-start(f32[8,1,24576]{2,1,0:T(1,128)} %reshape.300), calls=%async_computation.2 | async-start | bytes 1572864 | tf_op jit(solution)/shard_map/all_to_all | solution.py:179
  133.4 2.9 fusion.352
  136.2 2.9 fusion.354
  139.1 14.3 %all-to-all-done.2 = f32[8,1,24576]{2,1,0:T(1,128)} async-done(((f32[8,1,24576]{2,1,0:T(1,128)}), f32[8,1,24576]{2,1,0:T(1,128)}, u32[]{:S(2)}, u32[]{:S(2)}) %all-to-all-start.2) | async-done | bytes 786464 | tf_op jit(solution)/shard_map/all_to_all | solution.py:179
  153.4 3.7 reduce.2
  157.1 4.8 reshape.301
  161.9 6.4 %copy.353 = f32[2,3,16,16,8,16]{3,4,5,2,1,0:T(8,128)S(1)} copy(f32[2,3,16,16,8,16]{3,2,1,0,5,4:T(8,128)} %bitcast.184) | data formatting | bytes 1572864 | tf_op jit(solution)/shard_map/all_to_all | solution.py:179
  168.3 3.1 fusion.341
  171.4 2.4 squeeze.26
  174.6 2.9 squeeze.27
  179.7 6.0 %copy.300 = f32[2,3,16,16,128]{3,2,1,0,4:T(8,128)} copy(f32[2,3,16,16,128]{4,3,2,1,0:T(8,128)S(1)} %pad_maximum_fusion.9) | data formatting | bytes 1572864 | tf_op jit(solution)/shard_map/stack | solution.py:62
  185.7 5.5 %reshape.302 = f32[4,1,49152]{2,1,0:T(1,128)} reshape(f32[128,2,3,16,16]{4,3,2,1,0:T(8,128)} %bitcast.185) | data formatting | bytes 1572864
  191.2 4.2 all-to-all-start.3
  197.1 2.8 fusion.356
  199.9 5.9 %all-to-all-done.3 = f32[4,1,49152]{2,1,0:T(1,128)} async-done(((f32[4,1,49152]{2,1,0:T(1,128)}), f32[4,1,49152]{2,1,0:T(1,128)}, u32[]{:S(2)}, u32[]{:S(2)}) %all-to-all-start.3) | async-done | bytes 786464 | tf_op jit(solution)/shard_map/all_to_all | solution.py:185
  205.8 3.9 reduce.3
  209.6 4.9 %reshape.303 = f32[128,2,3,16,16]{4,3,2,1,0:T(8,128)} reshape(f32[4,49152]{1,0:T(4,128)S(1)} %reduce.3) | data formatting | bytes 1572864
  214.5 6.7 %copy.301 = f32[2,3,16,16,4,32]{5,3,2,4,1,0:T(8,128)} copy(f32[2,3,16,16,4,32]{3,2,1,0,5,4:T(8,128)} %bitcast.186) | data formatting | bytes 1572864 | tf_op jit(solution)/shard_map/all_to_all | solution.py:185
  221.2 3.8 fusion.343
  225.0 2.9 copy.303
  227.9 2.0 copy.302
  242.0 2.6 copy.342
  244.6 2.5 copy.344
  247.2 2.5 copy.346
  249.7 2.6 copy.347
  252.2 2.5 copy.349
  254.8 2.5 copy.351
  267.1 40.1 %pmax.7 = f32[]{:T(128)} all-reduce(f32[]{:T(128)} %get-tuple-element.5), channel_id=1, replica_groups=mesh['row'=4,'col'=8] {'row','col'}, use_global_device_ids=true, to_apply=%region_1.2 | all-reduce | flops 1 | bytes 8 | tf_op jit(solution)/shard_map/pmax | solution.py:189
  312.0 9.8 %copy.310 = f32[3,34,18,128,2]{1,4,3,2,0:T(2,128)} copy(f32[3,34,18,128,2]{3,1,2,0,4:T(8,128)} %pad_maximum_fusion.3) | data formatting | bytes 3760128 | tf_op jit(solution)/shard_map/stack | solution.py:99
  321.8 12.1 %fusion.3 = (f32[3,32,1,18,256]{1,4,3,0,2:T(8,128)}, f32[3,32,1,18,256]{1,4,3,0,2:T(8,128)}) fusion(f32[3,34,18,256]{1,3,2,0:T(8,128)} %bitcast.175), kind=kLoop, calls=%fused_computation.6 | loop fusion | flops 2211840 | bytes 8847360 | tf_op jit(solution)/shard_map/stack | solution.py:109
  333.9 12.6 %pad_maximum_fusion = f32[3,32,2,18,256]{1,4,3,0,2:T(8,128)} fusion(f32[3,32,1,18,256]{1,4,3,0,2:T(8,128)} %get-tuple-element.8, f32[3,32,1,18,256]{1,4,3,0,2:T(8,128)} %get-tuple-element.7), kind=kLoop, calls=%fused_computation | loop fusion | flops 884736 | bytes 7077888 | tf_op jit(solution)/shard_map/stack | solution.py:109
  346.5 11.0 %copy.311 = f32[3,32,2,18,256]{4,2,1,3,0:T(2,128)} copy(f32[3,32,2,18,256]{1,4,3,0,2:T(8,128)} %pad_maximum_fusion) | data formatting | bytes 7077888 | tf_op jit(solution)/shard_map/stack | solution.py:109
  357.5 5.8 %reshape.287 = f32[3,64,18,256]{3,1,2,0:T(8,128)} reshape(f32[3,32,2,18,256]{4,2,1,3,0:T(2,128)} %copy.311) | data formatting | bytes 7077888 | tf_op jit(solution)/shard_map/reshape | solution.py:109
  363.3 4.8 %fusion.7 = (f32[3,64,16,1,256]{4,1,2,0,3:T(8,128)S(1)}, f32[3,64,16,1,256]{4,1,2,0,3:T(8,128)S(1)}) fusion(f32[3,64,18,256]{3,1,2,0:T(8,128)} %reshape.287), kind=kLoop, calls=%fused_computation.18 | loop fusion | flops 3932160 | bytes 15728640 | tf_op jit(solution)/shard_map/stack | solution.py:109
  380.5 23.9 %fusion.21 = f32[1,64,32,256]{3,1,2,0:T(8,128)S(1)} fusion(f32[64,32,3]{2,0,1:T(8,128)S(1)} %copy-done.15, f32[64,32,253]{2,0,1:T(8,128)S(1)} %copy-done.9, f32[64,32,2]{2,0,1:T(8,128)S(1)} %copy-done.16, f32[64,32,254]{2,0,1:T(8,128)S(1)} %copy-done.10, f32[64,32,1]{2,0,1:T(8,128)S(1)} %copy-done.17, f32[64,32,255]{2,0,1:T(8,128)S(1)} %copy-done.11, ...), kind=kLoop, calls=%fused_computation.57 | loop fusion | flops 152567808 | bytes 31457280 | tf_op jit(solution)/shard_map/stack | solution.py:196
  404.4 2.1 collective-permute-start.4
  406.8 5.2 %collective-permute-done.4 = f32[2,3,32,256]{3,1,2,0:T(4,128)S(1)} collective-permute-done((f32[2,3,32,256]{3,1,2,0:T(4,128)S(1)}, f32[2,3,32,256]{3,1,2,0:T(4,128)S(1)}, u32[]{:S(2)}, u32[]{:S(2)}) %collective-permute-start.4) | collective-permute-done | bytes 196640 | tf_op jit(solution)/shard_map/ppermute | solution.py:21
  412.0 6.3 %collective-permute-done.5 = f32[2,3,32,256]{3,1,2,0:T(4,128)S(1)} collective-permute-done((f32[2,3,32,256]{3,1,2,0:T(4,128)S(1)}, f32[2,3,32,256]{3,1,2,0:T(4,128)S(1)}, u32[]{:S(2)}, u32[]{:S(2)}) %collective-permute-start.5) | collective-permute-done | bytes 196640 | tf_op jit(solution)/shard_map/ppermute | solution.py:19
  419.8 20.3 %fusion.76 = f32[1,64,32,256]{3,1,2,0:T(8,128)S(1)} fusion(f32[1,64,32,256]{3,1,2,0:T(8,128)S(1)} %fusion.21, f32[2,67,32,256]{3,1,2,0:T(8,128)S(1)} %get-tuple-element.21, f32[2,67,32,256]{3,1,2,0:T(8,128)S(1)} %get-tuple-element.20, f32[1,64,32,256]{3,1,2,0:T(8,128)S(1)} %bitcast.178), kind=kLoop, calls=%fused_computation.112 | loop fusion | flops 146276352 | bytes 31457280 | tf_op jit(solution)/shard_map/add | solution.py:129
  440.2 4.8 %collective-permute-start.6 = (f32[2,64,3,256]{3,1,2,0:T(8,128)S(1)}, f32[2,64,3,256]{3,1,2,0:T(8,128)S(1)}, u32[]{:S(2)}, u32[]{:S(2)}) collective-permute-start(f32[2,64,3,256]{3,1,2,0:T(8,128)S(1)} %get-tuple-element.18), channel_id=1, source_target_pairs={{0,1},{1,2},{2,3},{3,4},{4,5},{5,6},{6,7},{7,0},{8,9},{9,10},{10,1... | collective-permute-start | bytes 1179656 | tf_op jit(solution)/shard_map/ppermute | solution.py:19
  445.0 7.7 %collective-permute-done.6 = f32[2,64,3,256]{3,1,2,0:T(8,128)S(1)} collective-permute-done((f32[2,64,3,256]{3,1,2,0:T(8,128)S(1)}, f32[2,64,3,256]{3,1,2,0:T(8,128)S(1)}, u32[]{:S(2)}, u32[]{:S(2)}) %collective-permute-start.6) | collective-permute-done | bytes 393248 | tf_op jit(solution)/shard_map/ppermute | solution.py:19
  452.7 2.7 collective-permute-done.7
  456.4 19.0 %fusion.131 = f32[64,32,256]{2,0,1:T(8,128)S(1)} fusion(f32[64,38,256]{2,0,1:T(8,128)S(1)} %get-tuple-element.17, f32[64,38,256]{2,0,1:T(8,128)S(1)} %get-tuple-element.16), kind=kLoop, calls=%fused_computation.167 | loop fusion | flops 146276352 | bytes 31457280 | tf_op jit(solution)/shard_map/add | solution.py:129
  475.4 2.5 copy.326
  (133 shorter events, 62.6 us)
Async XLA Ops:
  0.0 1.1 copy-start
  56.6 27.0 %all-to-all-start.1 = ((f32[8,1,24576]{2,1,0:T(1,128)}), f32[8,1,24576]{2,1,0:T(1,128)S(1)}, u32[]{:S(2)}, u32[]{:S(2)}) async-start(f32[8,1,24576]{2,1,0:T(1,128)} %reshape.298), calls=%async_computation.1 | async-start | bytes 1572864 | tf_op jit(solution)/shard_map/all_to_all | solution.py:156
  122.4 11.0 %copy-start.2 = (f32[64,32,256]{2,1,0:T(8,128)S(1)}, f32[64,32,256]{2,1,0:T(8,128)}, u32[]{:S(2)}) copy-start(f32[64,32,256]{2,1,0:T(8,128)} %param.3) | copy-start | bytes 6291460
  128.0 25.4 %all-to-all-start.2 = ((f32[8,1,24576]{2,1,0:T(1,128)}), f32[8,1,24576]{2,1,0:T(1,128)}, u32[]{:S(2)}, u32[]{:S(2)}) async-start(f32[8,1,24576]{2,1,0:T(1,128)} %reshape.300), calls=%async_computation.2 | async-start | bytes 1572864 | tf_op jit(solution)/shard_map/all_to_all | solution.py:179
  191.2 14.6 %all-to-all-start.3 = ((f32[4,1,49152]{2,1,0:T(1,128)}), f32[4,1,49152]{2,1,0:T(1,128)}, u32[]{:S(2)}, u32[]{:S(2)}) async-start(f32[4,1,49152]{2,1,0:T(1,128)} %reshape.302), calls=%async_computation.3 | async-start | bytes 1572864 | tf_op jit(solution)/shard_map/all_to_all | solution.py:185
  233.5 3.6 collective-permute-start
  234.3 2.8 collective-permute-start.1
  238.2 69.7 %collective-permute-start.2 = (f32[3,34,1,128]{3,1,0,2:T(8,128)S(1)}, f32[3,34,1,128]{3,1,0,2:T(8,128)S(1)}, u32[]{:S(2)}, u32[]{:S(2)}) collective-permute-start(f32[3,34,1,128]{3,1,0,2:T(8,128)S(1)} %get-tuple-element.60), channel_id=1, source_target_pairs={{0,1},{1,2},{2,3},{3,4},{4,5},{5,6},{6,7},{7,0},{8,9},{9,10},{10,1... | collective-permute-start | bytes 156680 | tf_op jit(solution)/shard_map/ppermute | solution.py:19
  240.0 2.1 copy-start.5
  240.0 68.0 %collective-permute-start.3 = (f32[3,34,1,128]{3,1,0,2:T(8,128)S(1)}, f32[3,34,1,128]{3,1,0,2:T(8,128)S(1)}, u32[]{:S(2)}, u32[]{:S(2)}) collective-permute-start(f32[3,34,1,128]{3,1,0,2:T(8,128)S(1)} %get-tuple-element.61), channel_id=1, source_target_pairs={{1,0},{2,1},{3,2},{4,3},{5,4},{6,5},{7,6},{0,7},{9,8},{10,9},{11,1... | collective-permute-start | bytes 156680 | tf_op jit(solution)/shard_map/ppermute | solution.py:21
  242.0 2.6 copy-start.6
  244.6 2.5 copy-start.8
  247.2 2.5 copy-start.7
  249.7 2.6 copy-start.4
  252.2 2.5 copy-start.3
  254.8 2.5 copy-start.22
  262.1 3.2 copy-start.21
  308.5 1.2 copy-start.23
  371.5 6.2 %copy-start.19 = (f32[64,32,2]{2,0,1:T(8,128)S(1)}, f32[64,32,2]{2,0,1:T(8,128)}, u32[]{:S(2)}) copy-start(f32[64,32,2]{2,0,1:T(8,128)} %copy.350) | copy-start | bytes 49156
  371.5 6.2 %copy-start.20 = (f32[64,32,3]{2,0,1:T(8,128)S(1)}, f32[64,32,3]{2,0,1:T(8,128)}, u32[]{:S(2)}) copy-start(f32[64,32,3]{2,0,1:T(8,128)} %copy.352) | copy-start | bytes 73732
  372.2 5.5 %copy-start.15 = (f32[64,32,3]{2,0,1:T(8,128)S(1)}, f32[64,32,3]{2,0,1:T(8,128)}, u32[]{:S(2)}) copy-start(f32[64,32,3]{2,0,1:T(8,128)} %copy.341) | copy-start | bytes 73732
  372.2 5.5 %copy-start.16 = (f32[64,32,2]{2,0,1:T(8,128)S(1)}, f32[64,32,2]{2,0,1:T(8,128)}, u32[]{:S(2)}) copy-start(f32[64,32,2]{2,0,1:T(8,128)} %copy.343) | copy-start | bytes 49156
  372.2 5.5 %copy-start.17 = (f32[64,32,1]{2,0,1:T(8,128)S(1)}, f32[64,32,1]{2,0,1:T(8,128)}, u32[]{:S(2)}) copy-start(f32[64,32,1]{2,0,1:T(8,128)} %copy.345) | copy-start | bytes 24580
  372.3 5.5 %copy-start.18 = (f32[64,32,1]{2,0,1:T(8,128)S(1)}, f32[64,32,1]{2,0,1:T(8,128)}, u32[]{:S(2)}) copy-start(f32[64,32,1]{2,0,1:T(8,128)} %copy.348) | copy-start | bytes 24580
  374.0 3.7 copy-start.13
  374.0 3.8 copy-start.14
  375.7 3.0 copy-start.11
  375.7 3.6 copy-start.12
  377.4 2.4 copy-start.9
  377.4 3.0 copy-start.10
  404.4 7.5 %collective-permute-start.4 = (f32[2,3,32,256]{3,1,2,0:T(4,128)S(1)}, f32[2,3,32,256]{3,1,2,0:T(4,128)S(1)}, u32[]{:S(2)}, u32[]{:S(2)}) collective-permute-start(f32[2,3,32,256]{3,1,2,0:T(4,128)S(1)} %get-tuple-element.22), channel_id=1, source_target_pairs={{8,0},{16,8},{24,16},{0,24},{9,1},{17,9},{25,17},{1,25},{10,2},{18... | collective-permute-start | bytes 589832 | tf_op jit(solution)/shard_map/ppermute | solution.py:21
  406.5 11.8 %collective-permute-start.5 = (f32[2,3,32,256]{3,1,2,0:T(4,128)S(1)}, f32[2,3,32,256]{3,1,2,0:T(4,128)S(1)}, u32[]{:S(2)}, u32[]{:S(2)}) collective-permute-start(f32[2,3,32,256]{3,1,2,0:T(4,128)S(1)} %get-tuple-element.23), channel_id=1, source_target_pairs={{0,8},{8,16},{16,24},{24,0},{1,9},{9,17},{17,25},{25,1},{2,10},{10... | collective-permute-start | bytes 589832 | tf_op jit(solution)/shard_map/ppermute | solution.py:19
  440.2 12.5 %collective-permute-start.6 = (f32[2,64,3,256]{3,1,2,0:T(8,128)S(1)}, f32[2,64,3,256]{3,1,2,0:T(8,128)S(1)}, u32[]{:S(2)}, u32[]{:S(2)}) collective-permute-start(f32[2,64,3,256]{3,1,2,0:T(8,128)S(1)} %get-tuple-element.18), channel_id=1, source_target_pairs={{0,1},{1,2},{2,3},{3,4},{4,5},{5,6},{6,7},{7,0},{8,9},{9,10},{10,1... | collective-permute-start | bytes 1179656 | tf_op jit(solution)/shard_map/ppermute | solution.py:19
  445.0 10.4 %collective-permute-start.7 = (f32[2,64,3,256]{3,1,2,0:T(8,128)S(1)}, f32[2,64,3,256]{3,1,2,0:T(8,128)S(1)}, u32[]{:S(2)}, u32[]{:S(2)}) collective-permute-start(f32[2,64,3,256]{3,1,2,0:T(8,128)S(1)} %get-tuple-element.19), channel_id=1, source_target_pairs={{1,0},{2,1},{3,2},{4,3},{5,4},{6,5},{7,6},{0,7},{9,8},{10,9},{11,1... | collective-permute-start | bytes 1179656 | tf_op jit(solution)/shard_map/ppermute | solution.py:21
  456.3 21.6 %copy-start.1 = (f32[3,32,16,128]{3,2,1,0:T(8,128)S(1)}, f32[3,32,16,128]{3,2,1,0:T(8,128)}, u32[]{:S(2)}) copy-start(f32[3,32,16,128]{3,2,1,0:T(8,128)} %param.2) | copy-start | bytes 2359300
where the time goes:
time: 483 us; the launch traced here: 478 us
  local copies, waits for them, and re-layouts  199 us (41%)
  other arithmetic  115 us (24%)
  waiting for transfers between devices  62.5 us (13%)
  blocking collectives  54.6 us (11%)
  starting transfers between devices  29.4 us (6%)
  matrix products  16 us (3%)
    unnamed x69, local copies, waits for them, and re-layouts  66.4 us
    pmax x1, blocking collectives, shards(): velocity_peak = lax.pmax(jnp.max(jnp.abs(velocity)), ('row', 'col'))  40.1 us
    add x2, other arithmetic, remesh_rim(): summed = summed + values * kernel_weight(offset - moved)  39.3 us
    another operation x3, other arithmetic, refine_rim(): jnp.stack([lower, upper], axis=grid_axis + 1)  29.5 us
    another operation x1, other arithmetic, shards(): rows_input = jnp.stack([swept, displaced[1]])  23.9 us
    all_to_all x1, waiting for transfers between devices, shards(): lax.all_to_all(spectrum, 'col', split_axis=4, concat_axis=2, tiled=True)  19.6 us
    another operation x3, local copies, waits for them, and re-layouts, rotate(): jnp.stack([real_cos - direction * imag_sin, imag_cos + direction * real_s...  18.6 us
    ppermute x4, waiting for transfers between devices, with_halo(): lax.ppermute(tail, axis, [(i, (i + 1) % count) for i in range(count)])  14.8 us
  transfers between devices with their start and end apart: 11, of which 8 were waited for; matrix products, arithmetic and copies ran while one was open for 8% of the time, Pallas kernels for 0%

commit v1 on v0

--- a/solution.py
+++ b/solution.py
@@ -7,6 +7,29 @@
 COURANT = 0.9
 EPSILON = 1e-06
 HIGHEST = lax.Precision.HIGHEST
+
+
+def in_blocks(x, dim, size):
+    before, after = (x.shape[:dim], x.shape[dim + 1 :])
+    return jnp.moveaxis(x.reshape(*before, size, -1, *after), dim, 0)
+
+
+def in_order(blocks, dim):
+    dims = list(blocks.shape[1:])
+    dims[dim] *= blocks.shape[0]
+    return jnp.moveaxis(blocks, 0, dim).reshape(dims)
+
+
+def exchange_directly(x, axis, split_dim, concat_dim):
+    size, index = (lax.axis_size(axis), lax.axis_index(axis))
+    tiles = in_blocks(x, split_dim, size)
+    out = tiles
+    for lap in range(1, size):
+        target, source = ((index + lap) % size, (index - lap) % size)
+        sent = lax.dynamic_index_in_dim(tiles, target, 0)
+        received = lax.ppermute(sent, axis, [(i, (i + lap) % size) for i in range(size)])
+        out = lax.dynamic_update_slice_in_dim(out, received, source, axis=0)
+    return in_order(out, concat_dim)
 
 
 def with_halo(cells, sides, width):
@@ -153,11 +176,7 @@
         -1.0,
     )
     spectrum = rotate(
-        lax.all_to_all(spectrum, "col", split_axis=4, concat_axis=2, tiled=True),
-        "czkq,zw->ckqw",
-        cos_full,
-        sin_full,
-        -1.0,
+        exchange_directly(spectrum, "col", 4, 2), "czkq,zw->ckqw", cos_full, sin_full, -1.0
     )
     first_count = spectrum.shape[2]
     second_count = spectrum.shape[3]

time: 483 us -> 712 us (1.47)
  local copies, waits for them, and re-layouts: 199 us -> 366 us
  starting transfers between devices: 29.4 us -> 73.4 us
  waiting for transfers between devices: 62.5 us -> 84.7 us
  blocking collectives: 54.6 us -> 40.1 us
  matrix products: 16 us -> 26 us
    dynamic_update_slice x0 -> x7, local copies, waits for them, and re-layouts: none -> 149 us  [exchange_directly(): out = lax.dynamic_update_slice_in_dim(out, received, source, axis=0)]
    all_to_all x1, starting transfers between devices: 5.35 us -> 41.8 us  [shards(): lax.all_to_all(inverse_z, 'col', split_axis=4, concat_axis=3, tiled=True)]
    ppermute x0 -> x7, waiting for transfers between devices: none -> 32.1 us  [exchange_directly(): lax.ppermute(sent, axis, [(i, (i + lap) % size) for i in range(size)])]
    dynamic_slice x0 -> x1, local copies, waits for them, and re-layouts: none -> 20.8 us  [exchange_directly(): sent = lax.dynamic_index_in_dim(tiles, target, 0)]
    all_to_all x1 -> x0, blocking collectives: 14.5 us -> none  [shards(): lax.all_to_all(forward, 'row', split_axis=4, concat_axis=2, tiled=True)]
    all_to_all x1, waiting for transfers between devices: 19.6 us -> 9.44 us  [shards(): lax.all_to_all(forward, 'row', split_axis=4, concat_axis=2, tiled=True)]
    dot_general x4, matrix products: 2.85 us -> 12.9 us  [rotate(): real_cos = jnp.einsum(formula, complex_pair[0], cosine, precision=HIGHEST)]
    ppermute x0 -> x7, starting transfers between devices: none -> 9.95 us  [exchange_directly(): lax.ppermute(sent, axis, [(i, (i + lap) % size) for i in range(size)])]
  transfers between devices with their start and end apart: 11 -> 18, of which waited for: 8 -> 11; matrix products, arithmetic and copies ran while one was open for 8% -> 23% of each run, Pallas kernels for 0% -> 0%
where the time goes in v1:
time: 712 us; the launch traced here: 703 us
  local copies, waits for them, and re-layouts  366 us (51%)
  other arithmetic  112 us (16%)
  waiting for transfers between devices  84.7 us (12%)
  starting transfers between devices  73.4 us (10%)
  blocking collectives  40.1 us (6%)
  matrix products  26 us (4%)
    dynamic_update_slice x7, local copies, waits for them, and re-layouts, exchange_directly(): out = lax.dynamic_update_slice_in_dim(out, received, source, axis=0)  149 us
    unnamed x72, local copies, waits for them, and re-layouts  62.3 us
    all_to_all x1, starting transfers between devices, shards(): lax.all_to_all(inverse_z, 'col', split_axis=4, concat_axis=3, tiled=True)  41.8 us
    pmax x1, blocking collectives, shards(): velocity_peak = lax.pmax(jnp.max(jnp.abs(velocity)), ('row', 'col'))  40.1 us
    add x2, other arithmetic, remesh_rim(): summed = summed + values * kernel_weight(offset - moved)  39.3 us
    ppermute x7, waiting for transfers between devices, exchange_directly(): lax.ppermute(sent, axis, [(i, (i + lap) % size) for i in range(size)])  32.1 us
    another operation x3, other arithmetic, refine_rim(): jnp.stack([lower, upper], axis=grid_axis + 1)  29.2 us
    another operation x1, other arithmetic, shards(): rows_input = jnp.stack([swept, displaced[1]])  24 us
  transfers between devices with their start and end apart: 18, of which 11 were waited for; matrix products, arithmetic and copies ran while one was open for 23% of the time, Pallas kernels for 0%

profile of v1, /device:TPU:1, one launch (start us, length us, event | category | flops | bytes accessed | tf_op | source)
XLA Modules:
  0.0 703.5 jit_solution(15469157962856147950)
XLA Ops:
  5.7 4.4 reshape.309
  10.1 4.6 all-to-all-start
  15.3 9.4 %all-to-all-done = f32[4,1,49152]{2,1,0:T(1,128)S(1)} async-done(((f32[4,1,49152]{2,1,0:T(1,128)}), f32[4,1,49152]{2,1,0:T(1,128)S(1)}, u32[]{:S(2)}, u32[]{:S(2)}) %all-to-all-start) | async-done | bytes 786464 | tf_op jit(solution)/shard_map/all_to_all | solution.py:172
  25.3 2.9 reduce
  28.3 2.7 reshape.310
  31.0 3.7 copy.293
  45.1 2.6 stack.85
  47.7 10.7 %convolution_subtract_fusion.3 = f32[3,16,16,128]{3,2,1,0:T(8,128)S(1)} fusion(f32[3,16,16,128]{3,2,1,0:T(8,128)S(1)} %convolution_multiply_fusion.3, f32[3,128,16,16]{1,3,2,0:T(8,128)S(1)} %squeeze.22), kind=kOutput, calls=%fused_computation.269 | convolution fusion | flops 151322624 | bytes 1179648 | tf_op jit(solution)/shard_map/cyzk,yq->czkq/dot_general | solution.py:81
  58.5 2.7 stack.84
  61.2 4.0 constant_dynamic-update-slice_fusion.1
  67.1 20.8 %dynamic-slice_bitcast_fusion = (f32[1,2,3,16,16,16]{5,0,4,3,2,1:T(1,128)S(1)}, f32[1,2,3,16,16,16]{5,0,4,3,2,1:T(1,128)S(1)}, f32[1,2,3,16,16,16]{5,0,4,3,2,1:T...) fusion(f32[2,3,16,16,8,16]{5,4,3,2,1,0:T(8,128)} %constant_dyna, ...), kind=kLoop, calls=%fused_computation.285 | loop fusion | bytes 1376284 | tf_op jit(solution)/shard_map/jit(dynamic_index_in_dim)/dynamic_slice | solution.py:29
  87.9 2.6 collective-permute-start
  93.3 2.6 collective-permute-start.4
  95.8 11.7 %collective-permute-done = f32[1,2,3,16,16,16]{5,0,4,3,2,1:T(1,128)S(1)} collective-permute-done((f32[1,2,3,16,16,16]{5,0,4,3,2,1:T(1,128)}, f32[1,2,3,16,16,16]{5,0,4,3,2,1:T(1,128)S(1)}, u32[]{:S(2)}, u32[]{:S(2)}) %collective-permute-start) | collective-permute-done | bytes 98336 | tf_op jit(solution)/shard_map/ppermute | solution.py:30
  109.6 17.3 %collective-permute-done.1 = f32[1,2,3,16,16,16]{5,0,4,3,2,1:T(1,128)S(1)} collective-permute-done((f32[1,2,3,16,16,16]{5,0,4,3,2,1:T(1,128)}, f32[1,2,3,16,16,16]{5,0,4,3,2,1:T(1,128)S(1)}, u32[]{:S(2)}, u32[]{:S(2)}) %collective-permute-start.1) | collective-permute-done | bytes 98336 | tf_op jit(solution)/shard_map/ppermute | solution.py:30
  127.8 21.3 %dynamic_update_slice.21 = f32[8,2,3,16,16,16]{5,0,4,3,2,1:T(8,128)} dynamic-update-slice(f32[8,2,3,16,16,16]{5,0,4,3,2,1:T(8,128)} %bitcast.15, f32[1,2,3,16,16,16]{5,0,4,3,2,1:T(1,128)} %copy-done.24, s32[]{:T(128)S(6)} %select_n.422, s32[]{:T(128)} %constant.385.clone.1, s32[]{:T(128)} %constant.385.clone.1, s32[]{:T(128)} %constant.385.clone.1, s32[]{:T(128)} %constant.385.clone.1, ...) | dynamic-update-slice | bytes 196612 | tf_op jit(solution)/shard_map/dynamic_update_slice | solution.py:31
  149.1 21.3 %dynamic_update_slice.22 = f32[8,2,3,16,16,16]{5,0,4,3,2,1:T(8,128)} dynamic-update-slice(f32[8,2,3,16,16,16]{5,0,4,3,2,1:T(8,128)} %dynamic_update_slice.21, f32[1,2,3,16,16,16]{5,0,4,3,2,1:T(1,128)} %copy-done.25, s32[]{:T(128)S(6)} %select_n.426, s32[]{:T(128)} %constant.385.clone.1, s32[]{:T(128)} %constant.385.clone.1, s32[]{:T(128)} %constant.385.clone.1, s32[]{:T(128)} %constant.385.clone.1, ...) | dynamic-update-slice | bytes 196612 | tf_op jit(solution)/shard_map/dynamic_update_slice | solution.py:31
  170.4 21.3 %dynamic_update_slice.23 = f32[8,2,3,16,16,16]{5,0,4,3,2,1:T(8,128)} dynamic-update-slice(f32[8,2,3,16,16,16]{5,0,4,3,2,1:T(8,128)} %dynamic_update_slice.22, f32[1,2,3,16,16,16]{5,0,4,3,2,1:T(1,128)} %collective-permute-done.2, s32[]{:T(128)S(6)} %select_n.430, s32[]{:T(128)} %constant.385.clone.1, s32[]{:T(128)} %constant.385.clone.1, s32[]{:T(128)} %constant.385.clone.1, s32[]{:T(128)} %constant.385.clone.1, ...) | dynamic-update-slice | bytes 196612 | tf_op jit(solution)/shard_map/dynamic_update_slice | solution.py:31
  191.8 3.0 collective-permute-done.3
  194.8 21.3 %dynamic_update_slice.24 = f32[8,2,3,16,16,16]{5,0,4,3,2,1:T(8,128)} dynamic-update-slice(f32[8,2,3,16,16,16]{5,0,4,3,2,1:T(8,128)} %dynamic_update_slice.23, f32[1,2,3,16,16,16]{5,0,4,3,2,1:T(1,128)} %collective-permute-done.3, s32[]{:T(128)S(6)} %select_n.434, s32[]{:T(128)} %constant.385.clone.1, s32[]{:T(128)} %constant.385.clone.1, s32[]{:T(128)} %constant.385.clone.1, s32[]{:T(128)} %constant.385.clone.1, ...) | dynamic-update-slice | bytes 196612 | tf_op jit(solution)/shard_map/dynamic_update_slice | solution.py:31
  216.1 21.3 %dynamic_update_slice.25 = f32[8,2,3,16,16,16]{5,0,4,3,2,1:T(8,128)} dynamic-update-slice(f32[8,2,3,16,16,16]{5,0,4,3,2,1:T(8,128)} %dynamic_update_slice.24, f32[1,2,3,16,16,16]{5,0,4,3,2,1:T(1,128)} %collective-permute-done.4, s32[]{:T(128)S(6)} %select_n.438, s32[]{:T(128)} %constant.385.clone.1, s32[]{:T(128)} %constant.385.clone.1, s32[]{:T(128)} %constant.385.clone.1, s32[]{:T(128)} %constant.385.clone.1, ...) | dynamic-update-slice | bytes 196612 | tf_op jit(solution)/shard_map/dynamic_update_slice | solution.py:31
  237.4 21.3 %dynamic_update_slice.26 = f32[8,2,3,16,16,16]{5,0,4,3,2,1:T(8,128)} dynamic-update-slice(f32[8,2,3,16,16,16]{5,0,4,3,2,1:T(8,128)} %dynamic_update_slice.25, f32[1,2,3,16,16,16]{5,0,4,3,2,1:T(1,128)} %collective-permute-done.5, s32[]{:T(128)S(6)} %select_n.442, s32[]{:T(128)} %constant.385.clone.1, s32[]{:T(128)} %constant.385.clone.1, s32[]{:T(128)} %constant.385.clone.1, s32[]{:T(128)} %constant.385.clone.1, ...) | dynamic-update-slice | bytes 196612 | tf_op jit(solution)/shard_map/dynamic_update_slice | solution.py:31
  258.8 21.3 %dynamic_update_slice.27 = f32[8,2,3,16,16,16]{5,0,4,3,2,1:T(8,128)} dynamic-update-slice(f32[8,2,3,16,16,16]{5,0,4,3,2,1:T(8,128)} %dynamic_update_slice.26, f32[1,2,3,16,16,16]{5,0,4,3,2,1:T(1,128)} %collective-permute-done.6, s32[]{:T(128)S(6)} %select_n.446, s32[]{:T(128)} %constant.385.clone.1, s32[]{:T(128)} %constant.385.clone.1, s32[]{:T(128)} %constant.385.clone.1, s32[]{:T(128)} %constant.385.clone.1, ...) | dynamic-update-slice | bytes 196612 | tf_op jit(solution)/shard_map/dynamic_update_slice | solution.py:31
  280.1 6.3 fusion.340
  286.4 4.3 copy.297
  293.9 4.3 copy.296
  298.2 2.6 squeeze.24
  306.1 5.9 copy.298
  312.0 5.6 reshape.311
  317.6 41.8 %all-to-all-start.1 = ((f32[8,1,24576]{2,1,0:T(1,128)}), f32[8,1,24576]{2,1,0:T(1,128)}, u32[]{:S(2)}, u32[]{:S(2)}) async-start(f32[8,1,24576]{2,1,0:T(1,128)} %reshape.311), calls=%async_computation.1 | async-start | bytes 1572864 | tf_op jit(solution)/shard_map/all_to_all | solution.py:198
  359.4 2.8 fusion.350
  362.2 2.7 fusion.352
  364.9 14.5 %all-to-all-done.1 = f32[8,1,24576]{2,1,0:T(1,128)} async-done(((f32[8,1,24576]{2,1,0:T(1,128)}), f32[8,1,24576]{2,1,0:T(1,128)}, u32[]{:S(2)}, u32[]{:S(2)}) %all-to-all-start.1) | async-done | bytes 786464 | tf_op jit(solution)/shard_map/all_to_all | solution.py:198
  379.4 3.7 reduce.1
  383.1 4.7 reshape.312
  387.9 6.4 copy.353
  394.3 3.1 fusion.339
  400.5 2.6 squeeze.27
  405.3 5.9 copy.300
  411.2 5.5 reshape.313
  416.7 4.2 all-to-all-start.2
  422.6 2.7 fusion.354
  425.3 6.0 all-to-all-done.2
  431.3 3.9 reduce.2
  435.2 4.8 reshape.314
  440.0 6.7 copy.301
  446.7 3.8 fusion.341
  450.5 2.8 copy.303
  475.2 2.6 copy.347
  492.9 40.1 %pmax.7 = f32[]{:T(128)} all-reduce(f32[]{:T(128)} %get-tuple-element.5), channel_id=1, replica_groups=mesh['row'=4,'col'=8] {'row','col'}, use_global_device_ids=true, to_apply=%region_1.2 | all-reduce | flops 1 | bytes 8 | tf_op jit(solution)/shard_map/pmax | solution.py:208
  537.8 9.8 %copy.310 = f32[3,34,18,128,2]{1,4,3,2,0:T(2,128)} copy(f32[3,34,18,128,2]{3,1,2,0,4:T(8,128)} %pad_maximum_fusion.3) | data formatting | bytes 3760128 | tf_op jit(solution)/shard_map/stack | solution.py:122
  547.6 11.8 %fusion.3 = (f32[3,32,1,18,256]{1,4,3,0,2:T(8,128)}, f32[3,32,1,18,256]{1,4,3,0,2:T(8,128)}) fusion(f32[3,34,18,256]{1,3,2,0:T(8,128)} %bitcast.187), kind=kLoop, calls=%fused_computation.6 | loop fusion | flops 2211840 | bytes 8847360 | tf_op jit(solution)/shard_map/stack | solution.py:132
  559.4 12.6 %pad_maximum_fusion = f32[3,32,2,18,256]{1,4,3,0,2:T(8,128)} fusion(f32[3,32,1,18,256]{1,4,3,0,2:T(8,128)} %get-tuple-element.8, f32[3,32,1,18,256]{1,4,3,0,2:T(8,128)} %get-tuple-element.7), kind=kLoop, calls=%fused_computation | loop fusion | flops 884736 | bytes 7077888 | tf_op jit(solution)/shard_map/stack | solution.py:132
  572.0 10.9 %copy.311 = f32[3,32,2,18,256]{4,2,1,3,0:T(2,128)} copy(f32[3,32,2,18,256]{1,4,3,0,2:T(8,128)} %pad_maximum_fusion) | data formatting | bytes 7077888 | tf_op jit(solution)/shard_map/stack | solution.py:132
  582.9 5.5 reshape.300
  588.4 4.8 fusion.7
  605.7 24.0 %fusion.21 = f32[1,64,32,256]{3,1,2,0:T(8,128)S(1)} fusion(f32[64,32,3]{2,0,1:T(8,128)S(1)} %copy-done.16, f32[64,32,253]{2,0,1:T(8,128)S(1)} %copy-done.10, f32[64,32,2]{2,0,1:T(8,128)S(1)} %copy-done.17, f32[64,32,254]{2,0,1:T(8,128)S(1)} %copy-done.11, f32[64,32,1]{2,0,1:T(8,128)S(1)} %copy-done.18, f32[64,32,255]{2,0,1:T(8,128)S(1)} %copy-done.12, ...), kind=kLoop, calls=%fused_computation.57 | loop fusion | flops 152567808 | bytes 31457280 | tf_op jit(solution)/shard_map/stack | solution.py:215
  632.1 5.2 collective-permute-done.11
  637.3 6.3 collective-permute-done.12
  645.1 20.3 %fusion.76 = f32[1,64,32,256]{3,1,2,0:T(8,128)S(1)} fusion(f32[1,64,32,256]{3,1,2,0:T(8,128)S(1)} %fusion.21, f32[2,67,32,256]{3,1,2,0:T(8,128)S(1)} %get-tuple-element.28, f32[2,67,32,256]{3,1,2,0:T(8,128)S(1)} %get-tuple-element.27, f32[1,64,32,256]{3,1,2,0:T(8,128)S(1)} %bitcast.190), kind=kLoop, calls=%fused_computation.112 | loop fusion | flops 146276352 | bytes 31457280 | tf_op jit(solution)/shard_map/add | solution.py:152
  665.5 4.8 collective-permute-start.13
  670.4 7.7 %collective-permute-done.13 = f32[2,64,3,256]{3,1,2,0:T(8,128)S(1)} collective-permute-done((f32[2,64,3,256]{3,1,2,0:T(8,128)S(1)}, f32[2,64,3,256]{3,1,2,0:T(8,128)S(1)}, u32[]{:S(2)}, u32[]{:S(2)}) %collective-permute-start.13) | collective-permute-done | bytes 393248 | tf_op jit(solution)/shard_map/ppermute | solution.py:42
  678.0 2.7 collective-permute-done.14
  681.7 19.0 %fusion.131 = f32[64,32,256]{2,0,1:T(8,128)S(1)} fusion(f32[64,38,256]{2,0,1:T(8,128)S(1)} %get-tuple-element.24, f32[64,38,256]{2,0,1:T(8,128)S(1)} %get-tuple-element.23), kind=kLoop, calls=%fused_computation.167 | loop fusion | flops 146276352 | bytes 31457280 | tf_op jit(solution)/shard_map/add | solution.py:152
  (158 shorter events, 100.5 us)
Async XLA Ops:
  0.0 1.1 copy-start
  10.1 14.6 %all-to-all-start = ((f32[4,1,49152]{2,1,0:T(1,128)}), f32[4,1,49152]{2,1,0:T(1,128)S(1)}, u32[]{:S(2)}, u32[]{:S(2)}) async-start(f32[4,1,49152]{2,1,0:T(1,128)} %reshape.309), calls=%async_computation | async-start | bytes 1572864 | tf_op jit(solution)/shard_map/all_to_all | solution.py:172
  61.2 4.0 copy-start.3
  87.9 19.7 %collective-permute-start = (f32[1,2,3,16,16,16]{5,0,4,3,2,1:T(1,128)}, f32[1,2,3,16,16,16]{5,0,4,3,2,1:T(1,128)S(1)}, u32[]{:S(2)}, u32[]{:S(2)}) collective-permute-start(f32[1,2,3,16,16,16]{5,0,4,3,2,1:T(1,128)} %get-tuple-element.22), channel_id=1, source_target_pairs={{0,1},{1,2},{2,3},{3,4},{4,5},{5,6},{6,7},{7,0},{8,9},{9,10},{10,1... | collective-permute-start | bytes 294920 | tf_op jit(solution)/shard_map/ppermute | solution.py:30
  90.5 36.4 %collective-permute-start.1 = (f32[1,2,3,16,16,16]{5,0,4,3,2,1:T(1,128)}, f32[1,2,3,16,16,16]{5,0,4,3,2,1:T(1,128)S(1)}, u32[]{:S(2)}, u32[]{:S(2)}) collective-permute-start(f32[1,2,3,16,16,16]{5,0,4,3,2,1:T(1,128)} %get-tuple-element.21), channel_id=1, source_target_pairs={{0,2},{1,3},{2,4},{3,5},{4,6},{5,7},{6,0},{7,1},{8,10},{9,11},{10,... | collective-permute-start | bytes 294920 | tf_op jit(solution)/shard_map/ppermute | solution.py:30
  91.9 78.6 %collective-permute-start.2 = (f32[1,2,3,16,16,16]{5,0,4,3,2,1:T(1,128)}, f32[1,2,3,16,16,16]{5,0,4,3,2,1:T(1,128)}, u32[]{:S(2)}, u32[]{:S(2)}) collective-permute-start(f32[1,2,3,16,16,16]{5,0,4,3,2,1:T(1,128)} %get-tuple-element.20), channel_id=1, source_target_pairs={{0,3},{1,4},{2,5},{3,6},{4,7},{5,0},{6,1},{7,2},{8,11},{9,12},{10,... | collective-permute-start | bytes 294920 | tf_op jit(solution)/shard_map/ppermute | solution.py:30
  93.2 101.6 %collective-permute-start.3 = (f32[1,2,3,16,16,16]{5,0,4,3,2,1:T(1,128)S(1)}, f32[1,2,3,16,16,16]{5,0,4,3,2,1:T(1,128)}, u32[]{:S(2)}, u32[]{:S(2)}) collective-permute-start(f32[1,2,3,16,16,16]{5,0,4,3,2,1:T(1,128)S(1)} %get-tuple-element.19), channel_id=1, source_target_pairs={{0,4},{1,5},{2,6},{3,7},{4,0},{5,1},{6,2},{7,3},{8,12},{9,13},{10,... | collective-permute-start | bytes 294920 | tf_op jit(solution)/shard_map/ppermute | solution.py:30
  93.3 122.9 %collective-permute-start.4 = (f32[1,2,3,16,16,16]{5,0,4,3,2,1:T(1,128)S(1)}, f32[1,2,3,16,16,16]{5,0,4,3,2,1:T(1,128)}, u32[]{:S(2)}, u32[]{:S(2)}) collective-permute-start(f32[1,2,3,16,16,16]{5,0,4,3,2,1:T(1,128)S(1)} %get-tuple-element.18), channel_id=1, source_target_pairs={{0,5},{1,6},{2,7},{3,0},{4,1},{5,2},{6,3},{7,4},{8,13},{9,14},{10,... | collective-permute-start | bytes 294920 | tf_op jit(solution)/shard_map/ppermute | solution.py:30
  107.6 19.3 %copy-start.24 = (f32[1,2,3,16,16,16]{5,0,4,3,2,1:T(1,128)}, f32[1,2,3,16,16,16]{5,0,4,3,2,1:T(1,128)S(1)}, u32[]{:S(2)}) copy-start(f32[1,2,3,16,16,16]{5,0,4,3,2,1:T(1,128)S(1)} %collective-permute-done) | copy-start | bytes 294916
  107.6 129.9 %collective-permute-start.5 = (f32[1,2,3,16,16,16]{5,0,4,3,2,1:T(1,128)S(1)}, f32[1,2,3,16,16,16]{5,0,4,3,2,1:T(1,128)}, u32[]{:S(2)}, u32[]{:S(2)}) collective-permute-start(f32[1,2,3,16,16,16]{5,0,4,3,2,1:T(1,128)S(1)} %get-tuple-element.17), channel_id=1, source_target_pairs={{0,6},{1,7},{2,0},{3,1},{4,2},{5,3},{6,4},{7,5},{8,14},{9,15},{10,... | collective-permute-start | bytes 294920 | tf_op jit(solution)/shard_map/ppermute | solution.py:30
  126.9 0.9 copy-start.25
  126.9 131.9 %collective-permute-start.6 = (f32[1,2,3,16,16,16]{5,0,4,3,2,1:T(1,128)S(1)}, f32[1,2,3,16,16,16]{5,0,4,3,2,1:T(1,128)}, u32[]{:S(2)}, u32[]{:S(2)}) collective-permute-start(f32[1,2,3,16,16,16]{5,0,4,3,2,1:T(1,128)S(1)} %get-tuple-element.16), channel_id=1, source_target_pairs={{0,7},{1,0},{2,1},{3,2},{4,3},{5,4},{6,5},{7,6},{8,15},{9,8},{10,9... | collective-permute-start | bytes 294920 | tf_op jit(solution)/shard_map/ppermute | solution.py:30
  312.0 47.4 %copy-start.2 = (f32[64,32,256]{2,1,0:T(8,128)S(1)}, f32[64,32,256]{2,1,0:T(8,128)}, u32[]{:S(2)}) copy-start(f32[64,32,256]{2,1,0:T(8,128)} %param.3) | copy-start | bytes 6291460
  317.6 61.8 %all-to-all-start.1 = ((f32[8,1,24576]{2,1,0:T(1,128)}), f32[8,1,24576]{2,1,0:T(1,128)}, u32[]{:S(2)}, u32[]{:S(2)}) async-start(f32[8,1,24576]{2,1,0:T(1,128)} %reshape.311), calls=%async_computation.1 | async-start | bytes 1572864 | tf_op jit(solution)/shard_map/all_to_all | solution.py:198
  416.7 14.6 %all-to-all-start.2 = ((f32[4,1,49152]{2,1,0:T(1,128)}), f32[4,1,49152]{2,1,0:T(1,128)}, u32[]{:S(2)}, u32[]{:S(2)}) async-start(f32[4,1,49152]{2,1,0:T(1,128)} %reshape.313), calls=%async_computation.2 | async-start | bytes 1572864 | tf_op jit(solution)/shard_map/all_to_all | solution.py:204
  458.9 3.6 collective-permute-start.7
  459.7 2.8 collective-permute-start.8
  463.7 70.0 %collective-permute-start.9 = (f32[3,34,1,128]{3,1,0,2:T(8,128)S(1)}, f32[3,34,1,128]{3,1,0,2:T(8,128)S(1)}, u32[]{:S(2)}, u32[]{:S(2)}) collective-permute-start(f32[3,34,1,128]{3,1,0,2:T(8,128)S(1)} %get-tuple-element.67), channel_id=1, source_target_pairs={{0,1},{1,2},{2,3},{3,4},{4,5},{5,6},{6,7},{7,0},{8,9},{9,10},{10,1... | collective-permute-start | bytes 156680 | tf_op jit(solution)/shard_map/ppermute | solution.py:42
  465.5 2.1 copy-start.6
  465.5 68.3 %collective-permute-start.10 = (f32[3,34,1,128]{3,1,0,2:T(8,128)S(1)}, f32[3,34,1,128]{3,1,0,2:T(8,128)S(1)}, u32[]{:S(2)}, u32[]{:S(2)}) collective-permute-start(f32[3,34,1,128]{3,1,0,2:T(8,128)S(1)} %get-tuple-element.68), channel_id=1, source_target_pairs={{1,0},{2,1},{3,2},{4,3},{5,4},{6,5},{7,6},{0,7},{9,8},{10,9},{11,1... | collective-permute-start | bytes 156680 | tf_op jit(solution)/shard_map/ppermute | solution.py:44
  467.5 2.6 copy-start.7
  470.1 2.5 copy-start.9
  472.6 2.5 copy-start.8
  475.2 2.6 copy-start.5
  477.8 2.5 copy-start.4
  480.3 2.5 copy-start.22
  487.7 3.2 copy-start.21
  534.2 1.2 copy-start.23
  596.6 6.2 copy-start.20
  597.4 5.4 copy-start.16
  597.4 5.4 copy-start.17
  597.4 5.4 copy-start.18
  597.4 5.4 copy-start.19
  599.1 3.7 copy-start.14
  599.1 3.8 copy-start.15
  600.8 3.0 copy-start.12
  600.8 3.6 copy-start.13
  602.6 2.5 copy-start.10
  602.6 3.1 copy-start.11
  629.7 7.6 %collective-permute-start.11 = (f32[2,3,32,256]{3,1,2,0:T(4,128)S(1)}, f32[2,3,32,256]{3,1,2,0:T(4,128)S(1)}, u32[]{:S(2)}, u32[]{:S(2)}) collective-permute-start(f32[2,3,32,256]{3,1,2,0:T(4,128)S(1)} %get-tuple-element.29), channel_id=1, source_target_pairs={{8,0},{16,8},{24,16},{0,24},{9,1},{17,9},{25,17},{1,25},{10,2},{18... | collective-permute-start | bytes 589832 | tf_op jit(solution)/shard_map/ppermute | solution.py:44
  631.8 11.8 %collective-permute-start.12 = (f32[2,3,32,256]{3,1,2,0:T(4,128)S(1)}, f32[2,3,32,256]{3,1,2,0:T(4,128)S(1)}, u32[]{:S(2)}, u32[]{:S(2)}) collective-permute-start(f32[2,3,32,256]{3,1,2,0:T(4,128)S(1)} %get-tuple-element.30), channel_id=1, source_target_pairs={{0,8},{8,16},{16,24},{24,0},{1,9},{9,17},{17,25},{25,1},{2,10},{10... | collective-permute-start | bytes 589832 | tf_op jit(solution)/shard_map/ppermute | solution.py:42
  665.5 12.5 %collective-permute-start.13 = (f32[2,64,3,256]{3,1,2,0:T(8,128)S(1)}, f32[2,64,3,256]{3,1,2,0:T(8,128)S(1)}, u32[]{:S(2)}, u32[]{:S(2)}) collective-permute-start(f32[2,64,3,256]{3,1,2,0:T(8,128)S(1)} %get-tuple-element.25), channel_id=1, source_target_pairs={{0,1},{1,2},{2,3},{3,4},{4,5},{5,6},{6,7},{7,0},{8,9},{9,10},{10,1... | collective-permute-start | bytes 1179656 | tf_op jit(solution)/shard_map/ppermute | solution.py:42
  670.4 10.4 %collective-permute-start.14 = (f32[2,64,3,256]{3,1,2,0:T(8,128)S(1)}, f32[2,64,3,256]{3,1,2,0:T(8,128)S(1)}, u32[]{:S(2)}, u32[]{:S(2)}) collective-permute-start(f32[2,64,3,256]{3,1,2,0:T(8,128)S(1)} %get-tuple-element.26), channel_id=1, source_target_pairs={{1,0},{2,1},{3,2},{4,3},{5,4},{6,5},{7,6},{0,7},{9,8},{10,9},{11,1... | collective-permute-start | bytes 1179656 | tf_op jit(solution)/shard_map/ppermute | solution.py:44
  681.7 21.6 %copy-start.1 = (f32[3,32,16,128]{3,2,1,0:T(8,128)S(1)}, f32[3,32,16,128]{3,2,1,0:T(8,128)}, u32[]{:S(2)}) copy-start(f32[3,32,16,128]{3,2,1,0:T(8,128)} %param.2) | copy-start | bytes 2359300
